TPU v7x, 32 devices: a whole 2x2x4 slice. The times are simulated.
32 devices in a mesh: cls: 32 (over z, y, x, core).
Axes of the slice: x: 2, y: 2, z: 4, core: 2. Of those that a mesh axis runs over, the one named last changes fastest.
Arguments:
- features: bfloat16 [512, 12544], P('cls'), may hold values from -6 to 6
- fc_weight: bfloat16 [12544, 512], replicated, may hold values from -0.0546875 to 0.0546875
- centers: bfloat16 [131072, 512], P('cls'), may hold values from -6 to 6
- labels: int32 [512], replicated, may hold values from 0 to 131071
Outputs:
- loss: float32 [512], P('cls')
- grad_centers: bfloat16 [131072, 512], P('cls')
- grad_fc: float32 [12544, 512], P('cls')
All inputs are finite; a program needn't handle non-finite values.
Results may differ from a plain program's by a relative error of at most 0.0078.
Values may be sent and summed in bfloat16 or wider, within the bound.
A program may use at most 128 MiB of HBM per device.

v0:
```python
import math

import jax
import jax.numpy as jnp
from jax import lax
from jax.sharding import PartitionSpec as P

logit_scale = 64.0
cos_margin = math.cos(0.5)
sin_margin = math.sin(0.5)
epsilon = 1e-06


def inverse_norm(values):
    return lax.rsqrt(jnp.sum(values * values, axis=1, keepdims=True) + epsilon)


def margin_logits(emb_low, center_low, labels, offset):
    cosines = lax.dot_general(
        emb_low, center_low, (((1,), (1,)), ((), ())), preferred_element_type=jnp.float32
    )
    local_ids = labels - offset
    is_target = local_ids[:, None] == lax.broadcasted_iota(jnp.int32, (1, center_low.shape[0]), 1)
    target_cos = jnp.sum(jnp.where(is_target, cosines, 0.0), axis=1)
    target_sine = jnp.sqrt(1.0 - target_cos * target_cos)
    margined = target_cos * cos_margin - target_sine * sin_margin
    logits = logit_scale * jnp.where(is_target, margined[:, None], cosines)
    slope = cos_margin + sin_margin * target_cos / target_sine
    return (logits, is_target, slope)


def on_device(features, fc_weight, centers, labels):
    tok_rows = features.shape[0]
    class_rows = centers.shape[0]
    my_index = lax.axis_index("cls")
    columns = lax.all_to_all(features, "cls", split_axis=1, concat_axis=0, tiled=True)
    embedded = jnp.dot(features, fc_weight, preferred_element_type=jnp.float32).astype(jnp.bfloat16)
    gathered = lax.all_gather(embedded, "cls", axis=0, tiled=True)
    all_float = gathered.astype(jnp.float32)
    emb_low = (all_float * inverse_norm(all_float)).astype(jnp.bfloat16)
    own_float = embedded.astype(jnp.float32)
    inv_emb = inverse_norm(own_float)
    emb_dir = own_float * inv_emb
    center_float = centers.astype(jnp.float32)
    inv_center = inverse_norm(center_float)
    center_dir = center_float * inv_center
    center_low = center_dir.astype(jnp.bfloat16)
    logits, is_target, slope = margin_logits(emb_low, center_low, labels, my_index * class_rows)
    target_logit = jnp.sum(jnp.where(is_target, logits, 0.0), axis=1)
    row_total, target_all = lax.psum(
        (jnp.sum(jnp.exp(logits - logit_scale), axis=1), target_logit), "cls"
    )
    log_total = logit_scale + jnp.log(row_total)
    loss = lax.dynamic_slice_in_dim(log_total - target_all, my_index * tok_rows, tok_rows)
    probs = jnp.exp(logits - log_total[:, None])
    grad_cos = (
        logit_scale
        * (probs - is_target.astype(jnp.float32))
        * jnp.where(is_target, slope[:, None], 1.0)
    ).astype(jnp.bfloat16)
    grad_unit = lax.dot_general(
        grad_cos, emb_low, (((0,), (0,)), ((), ())), preferred_element_type=jnp.float32
    )
    grad_centers = (
        (grad_unit - center_dir * jnp.sum(grad_unit * center_dir, axis=1, keepdims=True))
        * inv_center
    ).astype(jnp.bfloat16)
    grad_dir = lax.psum_scatter(
        jnp.dot(grad_cos, center_low, preferred_element_type=jnp.float32),
        "cls",
        scatter_dimension=0,
        tiled=True,
    )
    grad_emb = (
        (grad_dir - emb_dir * jnp.sum(grad_dir * emb_dir, axis=1, keepdims=True)) * inv_emb
    ).astype(jnp.bfloat16)
    all_grads = lax.all_gather(grad_emb, "cls", axis=0, tiled=True)
    grad_fc = lax.dot_general(
        columns, all_grads, (((0,), (0,)), ((), ())), preferred_element_type=jnp.float32
    )
    return (loss, grad_centers, grad_fc)


def solution(mesh):
    placed = (P("cls", None), P(), P("cls", None), P())
    return jax.shard_map(
        on_device,
        mesh=mesh,
        in_specs=placed,
        out_specs=(P("cls"), P("cls", None), P("cls", None)),
        check_vma=False,
    )
```

profile of v0, /device:TPU:0, one launch (start us, length us, event | category | flops | bytes accessed | tf_op | source)
XLA Modules:
  0.0 323.5 jit_solution(14898361888110752312)
XLA Ops:
  7.2 2.2 all_to_all.14
  9.4 1.1 copy.10
  10.4 7.3 %all-to-all-start = ((bf16[16,32,392]{2,0,1:T(8,128)(2,1)}), bf16[16,32,392]{2,0,1:T(8,128)(2,1)S(1)}, u32[]{:S(2)}, u32[]{:S(2)}) async-start(bf16[16,32,392]{2,0,1:T(8,128)(2,1)} %copy.10), calls=%async_computation.1 | async-start | bytes 1048576 | tf_op jit(solution)/shard_map/all_to_all | solution.py:36
  17.8 0.0 reduce-scatter.2.cloned.1.call-start
  17.8 6.7 %fusion.23 = (f32[16]{0:T(128)S(1)}, bf16[16,512]{1,0:T(8,128)(2,1)S(1)}) fusion(bf16[16,12544]{1,0:T(8,128)(2,1)} %param.4, bf16[12544,512]{1,0:T(8,128)(2,1)} %param.5), kind=kOutput, calls=%fused_computation.33 | convolution fusion | flops 205553648 | bytes 13262912 | tf_op jit(solution)/shard_map/dot_general | solution.py:37
  24.5 0.0 copy-start.4
  24.5 43.2 %all_gather.6 = bf16[512,512]{1,0:T(8,128)(2,1)S(1)} all-gather(bf16[16,512]{1,0:T(8,128)(2,1)S(1)} %get-tuple-element.22), channel_id=1, replica_groups=mesh['cls'=32] {'cls'}, dimensions={0}, use_global_device_ids=true | all-gather | bytes 540672 | tf_op jit(solution)/shard_map/all_gather | solution.py:38
  67.7 0.2 fusion.12
  67.9 6.3 %copy.9 = bf16[4096,512]{0,1:T(8,128)(2,1)} copy(bf16[4096,512]{1,0:T(8,128)(2,1)} %param.6) | data formatting | bytes 8388608 | tf_op args[2]
  74.2 3.1 fusion.7
  77.3 0.0 copy-done.4
  77.3 4.9 %select_reduce_fusion.1 = (f32[512]{0:T(512)S(1)}, f32[512,4096]{1,0:T(8,128)S(1)}) fusion(s32[512]{0:T(512)S(1)} %broadcast_subtract_fusion, bf16[4096,512]{0,1:T(8,128)(2,1)} %copy.9, f32[4096]{0:T(1024)S(1)} %add_rsqrt_fusion, bf16[512,512]{1,0:T(8,128)(2,1)S(1)} %all_gather.6, f32[512]{0:T(512)S(1)} %add_rsqrt_fusion.1), kind=kOutput, calls=%fused_computation.14 | convolution fusion | flops 2160852480 | bytes 13129728 | tf_op jit(solution)/shard_map/dot_general | solution.py:19
  82.3 3.2 copy-done.2
  85.5 4.0 %exponential_reduce_fusion = (f32[512]{0:T(512)S(1)}, f32[512]{0:T(512)S(1)}) fusion(f32[512,4096]{1,0:T(8,128)S(1)} %get-tuple-element.18, f32[512]{0:T(512)S(1)} %get-tuple-element.16, s32[512]{0:T(512)S(1)} %broadcast_subtract_fusion), kind=kLoop, calls=%fused_computation.12 | loop fusion | flops 14679040 | bytes 8396800 | tf_op jit(solution)/shard_map/reduce_sum | solution.py:51
  89.5 37.0 %all-reduce = (f32[512]{0:T(512)S(1)}, f32[512]{0:T(512)S(1)}) all-reduce(f32[512]{0:T(512)S(1)} %get-tuple-element.10, f32[512]{0:T(512)S(1)} %get-tuple-element.9), channel_id=1, replica_groups=mesh['cls'=32] {'cls'}, use_global_device_ids=true, to_apply=%region_6.7 | all-reduce | flops 1024 | bytes 8192 | tf_op jit(solution)/shard_map/psum | solution.py:50
  126.6 6.8 %multiply_convert_fusion = bf16[512,4096]{1,0:T(8,128)(2,1)S(1)} fusion(f32[512,4096]{1,0:T(8,128)} %copy-done.2, f32[512]{0:T(512)S(1)} %get-tuple-element.15, f32[512]{0:T(512)S(1)} %get-tuple-element.13, f32[512]{0:T(512)S(1)} %get-tuple-element.16, s32[512]{0:T(512)S(1)} %broadcast_subtract_fusion), kind=kLoop, calls=%fused_computation.10 | loop fusion | flops 20971520 | bytes 12591104 | tf_op jit(solution)/shard_map/convert_element_type | solution.py:60
  133.4 0.0 copy-start.3
  133.4 1.9 copy-done.3
  135.3 0.0 copy-done
  135.3 3.3 %fusion.8 = f32[512,512]{1,0:T(8,128)} fusion(bf16[512,4096]{1,0:T(8,128)(2,1)S(1)} %multiply_convert_fusion, bf16[4096,512]{0,1:T(8,128)(2,1)S(1)} %copy-done, f32[4096]{0:T(1024)S(1)} %add_rsqrt_fusion), kind=kOutput, calls=%fused_computation.16 | convolution fusion | flops 2153775104 | bytes 9453568 | tf_op jit(solution)/shard_map/dot_general | solution.py:69
  138.6 0.0 reduce-scatter.2.cloned.1.call-update
  138.7 0.0 copy-start.1
  138.7 6.5 %fusion.3 = (f32[4096]{0:T(1024)S(1)}, f32[4096,512]{0,1:T(8,128)S(1)}) fusion(bf16[4096,512]{0,1:T(8,128)(2,1)} %copy.9, f32[4096]{0:T(1024)S(1)} %add_rsqrt_fusion, bf16[512,4096]{1,0:T(8,128)(2,1)} %copy-done.3, bf16[512,512]{1,0:T(8,128)(2,1)S(1)} %all_gather.6, f32[512]{0:T(512)S(1)} %add_rsqrt_fusion.1), kind=kOutput, calls=%fused_computation.5 | convolution fusion | flops 2156654592 | bytes 17336320 | tf_op jit(solution)/shard_map/dot_general | solution.py:61
  145.2 3.5 %fusion.6 = bf16[4096,512]{0,1:T(8,128)(2,1)} fusion(f32[4096,512]{0,1:T(8,128)S(1)} %get-tuple-element.20, bf16[4096,512]{0,1:T(8,128)(2,1)S(1)} %copy-done.1, f32[4096]{0:T(1024)S(1)} %get-tuple-element.19, f32[4096]{0:T(1024)S(1)} %add_rsqrt_fusion), kind=kLoop, calls=%fused_computation.8 | loop fusion | flops 12582912 | bytes 16809984 | tf_op jit(solution)/shard_map/convert_element_type | solution.py:67
  148.7 6.4 %copy.11 = bf16[4096,512]{1,0:T(8,128)(2,1)} copy(bf16[4096,512]{0,1:T(8,128)(2,1)} %fusion.6) | data formatting | bytes 8388608
  155.1 0.6 dynamic_slice.3
  155.7 120.1 %reduce-scatter.2.cloned.1.call-done = f32[16,512]{1,0:T(8,128)} async-done(((f32[512,512]{1,0:T(8,128)}), f32[16,512]{1,0:T(8,128)}) %reduce-scatter.2.cloned.1.call-update) | async-done | bytes 32784 | tf_op jit(solution)/shard_map/reduce_scatter | solution.py:68
  275.8 0.9 fusion.19
  276.8 0.8 fusion.22
  277.6 37.7 %all_gather.7 = bf16[512,512]{1,0:T(8,128)(2,1)S(1)} all-gather(bf16[16,512]{1,0:T(8,128)(2,1)S(1)} %fusion.22), channel_id=1, replica_groups=mesh['cls'=32] {'cls'}, dimensions={0}, use_global_device_ids=true | all-gather | bytes 540672 | tf_op jit(solution)/shard_map/all_gather | solution.py:77
  315.4 0.0 all-to-all-done
  315.4 1.3 convolution_bitcast_fusion
  (9 shorter events, 0.0 us)
Async XLA Ops:
  10.4 304.9 %all-to-all-start = ((bf16[16,32,392]{2,0,1:T(8,128)(2,1)}), bf16[16,32,392]{2,0,1:T(8,128)(2,1)S(1)}, u32[]{:S(2)}, u32[]{:S(2)}) async-start(bf16[16,32,392]{2,0,1:T(8,128)(2,1)} %copy.10), calls=%async_computation.1 | async-start | bytes 1048576 | tf_op jit(solution)/shard_map/all_to_all | solution.py:36
  17.8 258.1 %reduce-scatter.2.cloned.1.call-start = ((), (), s32[]{:S(2)}) async-start(), calls=%async_computation.2 | async-start | bytes 1081344 | tf_op jit(solution)/shard_map/reduce_scatter | solution.py:68
  24.5 52.8 %copy-start.4 = (s32[512]{0:T(512)S(1)}, s32[512]{0:T(512)}, u32[]{:S(2)}) copy-start(s32[512]{0:T(512)} %param.7) | copy-start | bytes 6148
  82.3 3.2 copy-start.2
  126.6 8.7 %copy-start = (bf16[4096,512]{0,1:T(8,128)(2,1)S(1)}, bf16[4096,512]{0,1:T(8,128)(2,1)}, u32[]{:S(2)}) copy-start(bf16[4096,512]{0,1:T(8,128)(2,1)} %copy.9) | copy-start | bytes 12582916
  133.4 1.9 copy-start.3
  138.7 6.5 %copy-start.1 = (bf16[4096,512]{0,1:T(8,128)(2,1)S(1)}, bf16[4096,512]{0,1:T(8,128)(2,1)}, u32[]{:S(2)}) copy-start(bf16[4096,512]{0,1:T(8,128)(2,1)} %copy.9) | copy-start | bytes 12582916
Sparse Core Ops, SparseCore 0:
  138.8 137.0 reduce-scatter.1
where the time goes:
time: 324 us
  waiting for transfers between devices  120 us (37%)
  blocking collectives  118 us (36%)
  matrix products  22.8 us (7%)
  local copies, waits for them, and re-layouts  21.7 us (7%)
  other arithmetic  19.4 us (6%)
  between operations  14.2 us (4%)
  starting transfers between devices  7.37 us (2%)
    reduce_scatter x1, waiting for transfers between devices, on_device(): lax.psum_scatter(jnp.dot(grad_cos, center_low, preferred_element_type=jnp...  120 us
    all_gather x1, blocking collectives, on_device(): gathered = lax.all_gather(embedded, 'cls', axis=0, tiled=True)  43.2 us
    all_gather x1, blocking collectives, on_device(): all_grads = lax.all_gather(grad_emb, 'cls', axis=0, tiled=True)  37.7 us
    psum x1, blocking collectives, on_device(): lax.psum((jnp.sum(jnp.exp(logits - logit_scale), axis=1), target_logit),...  37 us
    unnamed x12, local copies, waits for them, and re-layouts  17.9 us
    all_to_all x1, starting transfers between devices, on_device(): lax.all_to_all(features, 'cls', split_axis=1, concat_axis=0, tiled=True)  7.33 us
    convert_element_type x1, other arithmetic, on_device(): grad_cos = (logit_scale * (probs - is_target.astype(jnp.float32)) * jnp.w...  6.77 us
    dot_general x1, matrix products, on_device(): jnp.dot(features, fc_weight, preferred_element_type=jnp.float32)  6.67 us
  transfers between devices with their start and end apart: 2, of which 1 were waited for; matrix products, arithmetic and copies ran while one was open for 17% of the time, Pallas kernels for 0%

commit v1 on v0

--- a/solution.py
+++ b/solution.py
@@ -29,13 +29,22 @@
     return (logits, is_target, slope)
 
 
+def swap(blocks):
+    return lax.all_to_all(blocks, "cls", split_axis=0, concat_axis=0, tiled=True)
+
+
+def spread(block, count):
+    return swap(jnp.broadcast_to(block[None], (count, *block.shape)))
+
+
 def on_device(features, fc_weight, centers, labels):
     tok_rows = features.shape[0]
     class_rows = centers.shape[0]
     my_index = lax.axis_index("cls")
+    count = lax.axis_size("cls")
     columns = lax.all_to_all(features, "cls", split_axis=1, concat_axis=0, tiled=True)
     embedded = jnp.dot(features, fc_weight, preferred_element_type=jnp.float32).astype(jnp.bfloat16)
-    gathered = lax.all_gather(embedded, "cls", axis=0, tiled=True)
+    gathered = spread(embedded, count).reshape(count * tok_rows, -1)
     all_float = gathered.astype(jnp.float32)
     emb_low = (all_float * inverse_norm(all_float)).astype(jnp.bfloat16)
     own_float = embedded.astype(jnp.float32)
@@ -47,9 +56,8 @@
     center_low = center_dir.astype(jnp.bfloat16)
     logits, is_target, slope = margin_logits(emb_low, center_low, labels, my_index * class_rows)
     target_logit = jnp.sum(jnp.where(is_target, logits, 0.0), axis=1)
-    row_total, target_all = lax.psum(
-        (jnp.sum(jnp.exp(logits - logit_scale), axis=1), target_logit), "cls"
-    )
+    stats = jnp.stack([jnp.sum(jnp.exp(logits - logit_scale), axis=1), target_logit])
+    row_total, target_all = jnp.sum(spread(stats, count), axis=0)
     log_total = logit_scale + jnp.log(row_total)
     loss = lax.dynamic_slice_in_dim(log_total - target_all, my_index * tok_rows, tok_rows)
     probs = jnp.exp(logits - log_total[:, None])
@@ -65,16 +73,13 @@
         (grad_unit - center_dir * jnp.sum(grad_unit * center_dir, axis=1, keepdims=True))
         * inv_center
     ).astype(jnp.bfloat16)
-    grad_dir = lax.psum_scatter(
-        jnp.dot(grad_cos, center_low, preferred_element_type=jnp.float32),
-        "cls",
-        scatter_dimension=0,
-        tiled=True,
-    )
+    partial = jnp.dot(grad_cos, center_low, preferred_element_type=jnp.float32)
+    parts = swap(partial.astype(jnp.bfloat16).reshape(count, tok_rows, -1))
+    grad_dir = jnp.sum(parts.astype(jnp.float32), axis=0)
     grad_emb = (
         (grad_dir - emb_dir * jnp.sum(grad_dir * emb_dir, axis=1, keepdims=True)) * inv_emb
     ).astype(jnp.bfloat16)
-    all_grads = lax.all_gather(grad_emb, "cls", axis=0, tiled=True)
+    all_grads = spread(grad_emb, count).reshape(count * tok_rows, -1)
     grad_fc = lax.dot_general(
         columns, all_grads, (((0,), (0,)), ((), ())), preferred_element_type=jnp.float32
     )

time: 324 us -> 123 us (0.38)
  blocking collectives: 118 us -> 11 us
  waiting for transfers between devices: 120 us -> 25.6 us
  between operations: 14.2 us -> 0.8 us
  starting transfers between devices: 7.37 us -> 15.8 us
  other arithmetic: 19.4 us -> 23 us
    reduce_scatter x1 -> x0, waiting for transfers between devices: 120 us -> none  [on_device(): lax.psum_scatter(jnp.dot(grad_cos, center_low, preferred_element_type=jnp...]
    all_gather x2 -> x0, blocking collectives: 80.9 us -> none  [the longest x1 43.2 us: on_device(): gathered = lax.all_gather(embedded, 'cls', axis=0, tiled=True)]
    psum x1 -> x0, blocking collectives: 37 us -> none  [on_device(): lax.psum((jnp.sum(jnp.exp(logits - logit_scale), axis=1), target_logit),...]
    all_to_all x0 -> x3, waiting for transfers between devices: none -> 19.8 us  [swap(): lax.all_to_all(blocks, 'cls', split_axis=0, concat_axis=0, tiled=True)]
    all_to_all x0 -> x3, starting transfers between devices: none -> 12.9 us  [swap(): lax.all_to_all(blocks, 'cls', split_axis=0, concat_axis=0, tiled=True)]
    all_to_all x0 -> x1, blocking collectives: none -> 11 us  [swap(): lax.all_to_all(blocks, 'cls', split_axis=0, concat_axis=0, tiled=True)]
    all_to_all x1, waiting for transfers between devices: 0.01 us -> 5.81 us  [on_device(): lax.all_to_all(features, 'cls', split_axis=1, concat_axis=0, tiled=True)]
    convert_element_type x1, other arithmetic: 3.53 us -> 8.29 us  [on_device(): grad_centers = ((grad_unit - center_dir * jnp.sum(grad_unit * center_dir,...]
  transfers between devices with their start and end apart: 2 -> 4, of which waited for: 1 -> 4; matrix products, arithmetic and copies ran while one was open for 17% -> 29% of each run, Pallas kernels for 0% -> 0%
where the time goes in v1:
time: 123 us; the launch traced here: 122 us
  waiting for transfers between devices  25.6 us (21%)
  matrix products  25.5 us (21%)
  other arithmetic  23 us (19%)
  local copies, waits for them, and re-layouts  20.7 us (17%)
  starting transfers between devices  15.8 us (13%)
  blocking collectives  11 us (9%)
    all_to_all x3, waiting for transfers between devices, swap(): lax.all_to_all(blocks, 'cls', split_axis=0, concat_axis=0, tiled=True)  19.8 us
    unnamed x12, local copies, waits for them, and re-layouts  16 us
    all_to_all x3, starting transfers between devices, swap(): lax.all_to_all(blocks, 'cls', split_axis=0, concat_axis=0, tiled=True)  12.9 us
    all_to_all x1, blocking collectives, swap(): lax.all_to_all(blocks, 'cls', split_axis=0, concat_axis=0, tiled=True)  11 us
    dot_general x1, matrix products, on_device(): lax.dot_general(grad_cos, emb_low, (((0,), (0,)), ((), ())), preferred_el...  9.45 us
    convert_element_type x1, other arithmetic, on_device(): grad_centers = ((grad_unit - center_dir * jnp.sum(grad_unit * center_dir,...  8.29 us
    convert_element_type x1, other arithmetic, on_device(): grad_cos = (logit_scale * (probs - is_target.astype(jnp.float32)) * jnp.w...  6.78 us
    dot_general x1, matrix products, on_device(): jnp.dot(features, fc_weight, preferred_element_type=jnp.float32)  6.67 us
  transfers between devices with their start and end apart: 4, of which 4 were waited for; matrix products, arithmetic and copies ran while one was open for 29% of the time, Pallas kernels for 0%

profile of v1, /device:TPU:0, one launch (start us, length us, event | category | flops | bytes accessed | tf_op | source)
XLA Modules:
  0.0 122.4 jit_solution(10489114198073126917)
XLA Ops:
  0.6 6.7 %fusion.23 = (f32[16]{0:T(128)S(1)}, bf16[16,512]{1,0:T(8,128)(2,1)S(1)}) fusion(bf16[16,12544]{1,0:T(8,128)(2,1)} %param.4, bf16[12544,512]{1,0:T(8,128)(2,1)} %param.5), kind=kOutput, calls=%fused_computation.34 | convolution fusion | flops 205553648 | bytes 13262912 | tf_op jit(solution)/shard_map/dot_general | solution.py:46
  7.3 0.9 broadcast_in_dim.31
  8.2 7.3 %all-to-all-start = ((bf16[32,16,512]{2,1,0:T(8,128)(2,1)}), bf16[32,16,512]{2,1,0:T(8,128)(2,1)S(1)}, u32[]{:S(2)}, u32[]{:S(2)}) async-start(bf16[32,16,512]{2,1,0:T(8,128)(2,1)} %broadcast_in_dim.31), calls=%async_computation | async-start | bytes 1048576 | tf_op jit(solution)/shard_map/all_to_all | solution.py:33
  15.5 6.3 %copy.21 = bf16[4096,512]{0,1:T(8,128)(2,1)} copy(bf16[4096,512]{1,0:T(8,128)(2,1)} %param.6) | data formatting | bytes 8388608 | tf_op args[2]
  21.8 3.1 %fusion.7 = f32[4096]{0:T(1024)S(1)} fusion(bf16[4096,512]{0,1:T(8,128)(2,1)} %copy.21), kind=kLoop, calls=%fused_computation.9 | loop fusion | flops 6287360 | bytes 4210688 | tf_op jit(solution)/shard_map/reduce_sum | solution.py:15
  24.9 6.2 %all-to-all-done = bf16[32,16,512]{2,1,0:T(8,128)(2,1)S(1)} async-done(((bf16[32,16,512]{2,1,0:T(8,128)(2,1)}), bf16[32,16,512]{2,1,0:T(8,128)(2,1)S(1)}, u32[]{:S(2)}, u32[]{:S(2)}) %all-to-all-start) | async-done | bytes 524320 | tf_op jit(solution)/shard_map/all_to_all | solution.py:33
  31.1 0.2 multiply_reduce_fusion
  31.3 0.1 rsqrt.32
  31.4 0.2 fusion.15
  31.6 4.9 %select_reduce_fusion.1 = (f32[512]{0:T(512)S(1)}, f32[512,4096]{1,0:T(8,128)S(1)}) fusion(s32[512]{0:T(512)S(1)} %broadcast_subtract_fusion, bf16[512,512]{1,0:T(8,128)(2,1)S(1)} %fusion.15, bf16[4096,512]{0,1:T(8,128)(2,1)} %copy.21, f32[4096]{0:T(1024)S(1)} %add_rsqrt_fusion), kind=kOutput, calls=%fused_computation.14 | convolution fusion | flops 2160066048 | bytes 13127680 | tf_op jit(solution)/shard_map/dot_general | solution.py:19
  36.5 3.2 %copy-done.1 = f32[512,4096]{1,0:T(8,128)} copy-done((f32[512,4096]{1,0:T(8,128)}, f32[512,4096]{1,0:T(8,128)S(1)}, u32[]{:S(2)}) %copy-start.1) | copy-done | bytes 8388632
  39.7 4.0 %exponential_reduce_fusion = (f32[512]{0:T(512)S(1)}, f32[512]{0:T(512)S(1)}) fusion(f32[512,4096]{1,0:T(8,128)S(1)} %get-tuple-element.28, f32[512]{0:T(512)S(1)} %get-tuple-element.26, s32[512]{0:T(512)S(1)} %broadcast_subtract_fusion), kind=kLoop, calls=%fused_computation.12 | loop fusion | flops 14679040 | bytes 8396800 | tf_op jit(solution)/shard_map/reduce_sum | solution.py:59
  43.8 11.0 %all_to_all.36 = f32[32,2,512]{2,1,0:T(2,128)S(1)} all-to-all(f32[32,2,512]{2,1,0:T(2,128)S(1)} %broadcast_in_dim.34), channel_id=1, replica_groups=mesh['cls'=32] {'cls'}, dimensions={0} | all-to-all | bytes 262144 | tf_op jit(solution)/shard_map/all_to_all | solution.py:33
  54.9 6.8 %multiply_convert_fusion = bf16[512,4096]{1,0:T(8,128)(2,1)S(1)} fusion(f32[512,4096]{1,0:T(8,128)} %copy-done.1, f32[512]{0:T(512)S(1)} %get-tuple-element.25, f32[512]{0:T(512)S(1)} %bitcast.23, f32[512]{0:T(512)S(1)} %get-tuple-element.26, s32[512]{0:T(512)S(1)} %broadcast_subtract_fusion), kind=kLoop, calls=%fused_computation.10 | loop fusion | flops 20971520 | bytes 12591104 | tf_op jit(solution)/shard_map/convert_element_type | solution.py:68
  61.7 3.2 %fusion.12 = bf16[512,512]{1,0:T(8,128)(2,1)} fusion(bf16[512,4096]{1,0:T(8,128)(2,1)S(1)} %multiply_convert_fusion, bf16[4096,512]{0,1:T(8,128)(2,1)S(1)} %copy-done, f32[4096]{0:T(1024)S(1)} %add_rsqrt_fusion), kind=kOutput, calls=%fused_computation.19 | convolution fusion | flops 2154037248 | bytes 8929280 | tf_op jit(solution)/shard_map/dot_general | solution.py:76
  64.9 2.6 %all-to-all-start.2 = ((bf16[32,16,512]{2,1,0:T(8,128)(2,1)}), bf16[32,16,512]{2,1,0:T(8,128)(2,1)S(1)}, u32[]{:S(2)}, u32[]{:S(2)}) async-start(bf16[32,16,512]{2,1,0:T(8,128)(2,1)} %bitcast.5), calls=%async_computation.2 | async-start | bytes 1048576 | tf_op jit(solution)/shard_map/all_to_all | solution.py:33
  67.5 1.2 all_to_all.28
  68.7 1.1 copy.23
  69.9 13.3 %all-to-all-done.2 = bf16[32,16,512]{2,1,0:T(8,128)(2,1)S(1)} async-done(((bf16[32,16,512]{2,1,0:T(8,128)(2,1)}), bf16[32,16,512]{2,1,0:T(8,128)(2,1)S(1)}, u32[]{:S(2)}, u32[]{:S(2)}) %all-to-all-start.2) | async-done | bytes 524320 | tf_op jit(solution)/shard_map/all_to_all | solution.py:33
  83.1 2.9 %all-to-all-start.4 = ((bf16[16,32,392]{2,0,1:T(8,128)(2,1)}), bf16[16,32,392]{2,0,1:T(8,128)(2,1)S(1)}, u32[]{:S(2)}, u32[]{:S(2)}) async-start(bf16[16,32,392]{2,0,1:T(8,128)(2,1)} %copy.23), calls=%async_computation.4 | async-start | bytes 1048576 | tf_op jit(solution)/shard_map/all_to_all | solution.py:45
  86.0 9.5 %fusion.3 = (f32[4096]{0:T(1024)S(1)}, f32[4096,512]{0,1:T(8,128)}) fusion(bf16[4096,512]{0,1:T(8,128)(2,1)} %copy.21, f32[4096]{0:T(1024)S(1)} %add_rsqrt_fusion, bf16[512,4096]{1,0:T(8,128)(2,1)} %copy-done.2, bf16[512,512]{1,0:T(8,128)(2,1)S(1)} %fusion.15), kind=kOutput, calls=%fused_computation.5 | convolution fusion | flops 2155868160 | bytes 17334272 | tf_op jit(solution)/shard_map/dot_general | solution.py:69
  95.5 0.1 convert_reduce_fusion
  95.6 0.2 fusion.19
  95.8 0.1 fusion.22
  95.8 5.8 %all-to-all-done.4 = bf16[16,32,392]{2,0,1:T(8,128)(2,1)S(1)} async-done(((bf16[16,32,392]{2,0,1:T(8,128)(2,1)}), bf16[16,32,392]{2,0,1:T(8,128)(2,1)S(1)}, u32[]{:S(2)}, u32[]{:S(2)}) %all-to-all-start.4) | async-done | bytes 401440 | tf_op jit(solution)/shard_map/all_to_all | solution.py:45
  101.6 0.9 broadcast_in_dim.58
  102.5 3.0 %all-to-all-start.3 = ((bf16[32,16,512]{2,1,0:T(8,128)(2,1)}), bf16[32,16,512]{2,1,0:T(8,128)(2,1)S(1)}, u32[]{:S(2)}, u32[]{:S(2)}) async-start(bf16[32,16,512]{2,1,0:T(8,128)(2,1)} %broadcast_in_dim.58), calls=%async_computation.3 | async-start | bytes 1048576 | tf_op jit(solution)/shard_map/all_to_all | solution.py:33
  105.5 8.3 %fusion.6 = bf16[4096,512]{0,1:T(8,128)(2,1)} fusion(f32[4096,512]{0,1:T(8,128)} %get-tuple-element.30, bf16[4096,512]{0,1:T(8,128)(2,1)} %copy.21, f32[4096]{0:T(1024)S(1)} %get-tuple-element.29, f32[4096]{0:T(1024)S(1)} %add_rsqrt_fusion), kind=kLoop, calls=%fused_computation.8 | loop fusion | flops 12582912 | bytes 16809984 | tf_op jit(solution)/shard_map/convert_element_type | solution.py:75
  113.8 6.4 %copy.24 = bf16[4096,512]{1,0:T(8,128)(2,1)} copy(bf16[4096,512]{0,1:T(8,128)(2,1)} %fusion.6) | data formatting | bytes 8388608
  120.2 0.6 dynamic_slice.3
  120.7 0.3 all-to-all-done.3
  121.1 1.3 %convolution_bitcast_fusion = f32[392,512]{1,0:T(8,128)} fusion(bf16[32,16,512]{2,1,0:T(8,128)(2,1)S(1)} %all-to-all-done.3, bf16[16,32,392]{2,0,1:T(8,128)(2,1)S(1)} %all-to-all-done.4), kind=kOutput, calls=%fused_computation.18 | convolution fusion | flops 205520896 | bytes 1728512 | tf_op jit(solution)/shard_map/dot_general | solution.py:83
  (19 shorter events, 0.2 us)
Async XLA Ops:
  7.3 14.5 %copy-start.4 = (s32[512]{0:T(512)S(1)}, s32[512]{0:T(512)}, u32[]{:S(2)}) copy-start(s32[512]{0:T(512)} %param.7) | copy-start | bytes 6148
  8.2 22.9 %all-to-all-start = ((bf16[32,16,512]{2,1,0:T(8,128)(2,1)}), bf16[32,16,512]{2,1,0:T(8,128)(2,1)S(1)}, u32[]{:S(2)}, u32[]{:S(2)}) async-start(bf16[32,16,512]{2,1,0:T(8,128)(2,1)} %broadcast_in_dim.31), calls=%async_computation | async-start | bytes 1048576 | tf_op jit(solution)/shard_map/all_to_all | solution.py:33
  36.5 3.2 %copy-start.1 = (f32[512,4096]{1,0:T(8,128)}, f32[512,4096]{1,0:T(8,128)S(1)}, u32[]{:S(2)}) copy-start(f32[512,4096]{1,0:T(8,128)S(1)} %get-tuple-element.28) | copy-start | bytes 25165828
  54.9 6.8 %copy-start = (bf16[4096,512]{0,1:T(8,128)(2,1)S(1)}, bf16[4096,512]{0,1:T(8,128)(2,1)}, u32[]{:S(2)}) copy-start(bf16[4096,512]{0,1:T(8,128)(2,1)} %copy.21) | copy-start | bytes 12582916
  61.7 3.2 %copy-start.2 = (bf16[512,4096]{1,0:T(8,128)(2,1)}, bf16[512,4096]{1,0:T(8,128)(2,1)S(1)}, u32[]{:S(2)}) copy-start(bf16[512,4096]{1,0:T(8,128)(2,1)S(1)} %multiply_convert_fusion) | copy-start | bytes 12582916
  61.7 5.8 %copy-start.3 = (bf16[16,12544]{1,0:T(8,128)(2,1)S(1)}, bf16[16,12544]{1,0:T(8,128)(2,1)}, u32[]{:S(2)}) copy-start(bf16[16,12544]{1,0:T(8,128)(2,1)} %param.4) | copy-start | bytes 1204228
  64.9 18.2 %all-to-all-start.2 = ((bf16[32,16,512]{2,1,0:T(8,128)(2,1)}), bf16[32,16,512]{2,1,0:T(8,128)(2,1)S(1)}, u32[]{:S(2)}, u32[]{:S(2)}) async-start(bf16[32,16,512]{2,1,0:T(8,128)(2,1)} %bitcast.5), calls=%async_computation.2 | async-start | bytes 1048576 | tf_op jit(solution)/shard_map/all_to_all | solution.py:33
  83.1 18.5 %all-to-all-start.4 = ((bf16[16,32,392]{2,0,1:T(8,128)(2,1)}), bf16[16,32,392]{2,0,1:T(8,128)(2,1)S(1)}, u32[]{:S(2)}, u32[]{:S(2)}) async-start(bf16[16,32,392]{2,0,1:T(8,128)(2,1)} %copy.23), calls=%async_computation.4 | async-start | bytes 1048576 | tf_op jit(solution)/shard_map/all_to_all | solution.py:45
  102.5 18.6 %all-to-all-start.3 = ((bf16[32,16,512]{2,1,0:T(8,128)(2,1)}), bf16[32,16,512]{2,1,0:T(8,128)(2,1)S(1)}, u32[]{:S(2)}, u32[]{:S(2)}) async-start(bf16[32,16,512]{2,1,0:T(8,128)(2,1)} %broadcast_in_dim.58), calls=%async_computation.3 | async-start | bytes 1048576 | tf_op jit(solution)/shard_map/all_to_all | solution.py:33

commit v2 on v0

v2 whole, which is shorter than its diff:
```python
import functools
import math

import jax
import jax.numpy as jnp
from jax import lax
from jax.experimental import pallas as pl
from jax.experimental.pallas import tpu as pltpu
from jax.sharding import PartitionSpec as P

logit_scale = 64.0
cos_margin = math.cos(0.5)
sin_margin = math.sin(0.5)
epsilon = 1e-06
MESH = pl.DeviceIdType.MESH
f32, bf16 = jnp.float32, jnp.bfloat16


def inverse_norm(values):
    return lax.rsqrt(jnp.sum(values * values, axis=1, keepdims=True) + epsilon)


def largest_divisor(number, most):
    return next(d for d in range(most, 0, -1) if number % d == 0)


def kernel(
    n, rows, slots, feat, weight, centers_hbm, labels,
    loss_out, gc_out, cols_out, grads_out,
    wbuf, cbuf, clow, inv_c, cosines, acc, esend, emb, fsend, frecv,
    ssend, srecv, psend, precv, gsend, grecv, stage,
    wsem, csem, osem, ksem, ssems, rsems,
):
    me = lax.axis_index("cls")
    tok, feats = feat.shape
    classes, width = cbuf.shape
    batch = n * tok
    chunk = wbuf.shape[1]
    chunks = feats // chunk
    blocks = classes // rows
    part = feats // n
    half = n // 2

    def weight_copy(c):
        return pltpu.make_async_copy(
            weight.at[pl.ds(c * chunk, chunk)], wbuf.at[c % slots], wsem.at[c % slots]
        )

    for c in range(min(slots, chunks)):
        weight_copy(c).start()
    centers_copy = pltpu.make_async_copy(centers_hbm, cbuf, csem)
    centers_copy.start()

    barrier = pltpu.get_barrier_semaphore()

    def greet(i, carry):
        pl.semaphore_signal(barrier, inc=1, device_id=(lax.rem(me + i, n),), device_id_type=MESH)
        return carry

    lax.fori_loop(1, n, greet, 0)

    for j in range(n):
        fsend[j] = feat[:, j * part : (j + 1) * part]

    total = jnp.zeros((tok, width), f32)
    for c in range(chunks):
        weight_copy(c).wait()
        total = total + jnp.dot(
            feat[:, c * chunk : (c + 1) * chunk], wbuf[c % slots], preferred_element_type=f32
        )
        if c + slots < chunks:
            weight_copy(c + slots).start()
    esend[...] = total.astype(bf16)
    emb[me] = total.astype(bf16)
    pl.semaphore_wait(barrier, n - 1)

    def send_to(phase, source, target, first, last):
        def step(i, carry):
            dst = lax.rem(me + i, n)
            pltpu.make_async_remote_copy(
                src_ref=source(dst), dst_ref=target.at[me],
                send_sem=ssems.at[phase], recv_sem=rsems.at[phase],
                device_id=(dst,), device_id_type=MESH,
            ).start()
            return carry

        lax.fori_loop(first, last, step, 0)

    def wait_all(sems, phase, target):
        whole = target.at[pl.ds(0, n - 1)]
        pltpu.make_async_copy(whole, whole, sems.at[phase]).wait()

    send_to(0, lambda dst: esend, emb, 1, n)

    centers_copy.wait()

    def normalise(k, carry):
        at = pl.ds(pl.multiple_of(k * rows, rows), rows)
        block = cbuf[at].astype(f32)
        inv = inverse_norm(block)
        inv_c[at] = inv
        clow[at] = (block * inv).astype(bf16)
        return carry

    lax.fori_loop(0, blocks, normalise, 0)

    wait_all(rsems, 0, emb)
    send_to(1, lambda dst: fsend.at[dst], frecv, 1, half)
    frecv[me] = fsend[me]

    all_emb = emb[...].reshape(batch, width).astype(f32)
    emb_low = (all_emb * inverse_norm(all_emb)).astype(bf16)
    emb[...] = emb_low.reshape(n, tok, width)

    local = labels[...] - me * classes
    class_ids = lax.broadcasted_iota(jnp.int32, (rows, batch), 0)

    def forward(k, carry):
        esum, tcos = carry
        at = pl.ds(pl.multiple_of(k * rows, rows), rows)
        cos = lax.dot_general(
            clow[at], emb[...].reshape(batch, width), (((1,), (1,)), ((), ())),
            preferred_element_type=f32,
        )
        cosines[at] = cos
        hit = class_ids == local - k * rows
        tcos = tcos + jnp.sum(jnp.where(hit, cos, 0.0), axis=0, keepdims=True)
        powers = jnp.exp(logit_scale * cos - logit_scale)
        esum = esum + jnp.sum(jnp.where(hit, 0.0, powers), axis=0, keepdims=True)
        return esum, tcos

    zero_row = jnp.zeros((1, batch), f32)
    esum, tcos = lax.fori_loop(0, blocks, forward, (zero_row, zero_row))
    mine = (local >= 0) & (local < classes)
    tsin = jnp.sqrt(1.0 - tcos * tcos)
    tlogit = logit_scale * (tcos * cos_margin - tsin * sin_margin)
    slope = cos_margin + sin_margin * tcos / tsin
    esum = esum + jnp.where(mine, jnp.exp(tlogit - logit_scale), 0.0)
    ssend[0:1] = esum
    ssend[1:2] = jnp.where(mine, tlogit, 0.0)
    srecv[me] = ssend[...]
    send_to(2, lambda dst: ssend, srecv, 1, n)
    wait_all(rsems, 2, srecv)
    send_to(1, lambda dst: fsend.at[dst], frecv, half, n)
    stats = jnp.sum(srecv[...], axis=0)
    log_total = logit_scale + jnp.log(stats[0:1])
    loss_out[...] = log_total - stats[1:2]
    tgrad = logit_scale * (jnp.exp(tlogit - log_total) - 1.0) * slope

    def grad_cos(k):
        at = pl.ds(pl.multiple_of(k * rows, rows), rows)
        hit = class_ids == local - k * rows
        probs = jnp.exp(logit_scale * cosines[at] - log_total)
        return jnp.where(hit, tgrad, logit_scale * probs).astype(bf16)

    acc[...] = jnp.zeros_like(acc)

    def embed_grads(k, carry):
        at = pl.ds(pl.multiple_of(k * rows, rows), rows)
        acc[...] += lax.dot_general(
            grad_cos(k), clow[at], (((0,), (0,)), ((), ())), preferred_element_type=f32
        )
        return carry

    lax.fori_loop(0, blocks, embed_grads, 0)
    psend[...] = acc[...].astype(bf16).reshape(n, tok, width)
    precv[me] = psend[me]
    send_to(3, lambda dst: psend.at[dst], precv, 1, n)

    def out_copy(k, slot):
        at = pl.ds(pl.multiple_of(k * rows, rows), rows)
        return pltpu.make_async_copy(stage.at[slot], gc_out.at[at], osem.at[slot])

    def center_grads(k, carry):
        at = pl.ds(pl.multiple_of(k * rows, rows), rows)
        unit = jnp.dot(
            grad_cos(k), emb[...].reshape(batch, width), preferred_element_type=f32
        )
        inv = inv_c[at]
        direction = cbuf[at].astype(f32) * inv
        along = jnp.sum(unit * direction, axis=1, keepdims=True)
        slot = lax.rem(k, 2)

        @pl.when(k >= 2)
        def _():
            out_copy(k - 2, slot).wait()

        stage[slot] = ((unit - direction * along) * inv).astype(bf16)
        out_copy(k, slot).start()
        return carry

    lax.fori_loop(0, blocks, center_grads, 0)

    wait_all(rsems, 3, precv)
    grad_dir = jnp.sum(precv[...].astype(f32), axis=0)
    own = esend[...].astype(f32)
    inv_emb = inverse_norm(own)
    emb_dir = own * inv_emb
    along = jnp.sum(grad_dir * emb_dir, axis=1, keepdims=True)
    grad_emb = ((grad_dir - emb_dir * along) * inv_emb).astype(bf16)
    gsend[...] = grad_emb
    grecv[me] = grad_emb
    send_to(4, lambda dst: gsend, grecv, 1, n)

    wait_all(rsems, 1, frecv)
    cols_copy = pltpu.make_async_copy(frecv, cols_out, ksem.at[0])
    cols_copy.start()
    for k in range(max(blocks - 2, 0), blocks):
        out_copy(k, k % 2).wait()
    wait_all(rsems, 4, grecv)
    grads_copy = pltpu.make_async_copy(grecv, grads_out, ksem.at[1])
    grads_copy.start()
    for phase, target in ((0, emb), (1, frecv), (2, srecv), (3, precv), (4, grecv)):
        wait_all(ssems, phase, target)
    cols_copy.wait()
    grads_copy.wait()


def on_device(features, fc_weight, centers, labels):
    n = lax.axis_size("cls")
    tok, feats = features.shape
    classes, width = centers.shape
    batch = labels.shape[0]
    rows = min(512, 262144 // batch)
    slots = 4 if batch <= 1024 else 2
    chunk = feats // 128 // 7 * 128
    chunk = 128 * largest_divisor(feats // 128, 14)
    part = feats // n
    vmem = pl.BlockSpec(memory_space=pltpu.VMEM)
    hbm = pl.BlockSpec(memory_space=pl.ANY)
    loss_row, grad_centers, columns, all_grads = pl.pallas_call(
        functools.partial(kernel, n, rows, slots),
        out_shape=(
            jax.ShapeDtypeStruct((1, batch), f32),
            jax.ShapeDtypeStruct((classes, width), bf16),
            jax.ShapeDtypeStruct((n, tok, part), bf16),
            jax.ShapeDtypeStruct((n, tok, width), bf16),
        ),
        in_specs=[vmem, hbm, hbm, vmem],
        out_specs=(vmem, hbm, hbm, hbm),
        scratch_shapes=[
            pltpu.VMEM((slots, chunk, width), bf16),
            pltpu.VMEM((classes, width), bf16),
            pltpu.VMEM((classes, width), bf16),
            pltpu.VMEM((classes, 1), f32),
            pltpu.VMEM((classes, batch), f32),
            pltpu.VMEM((batch, width), f32),
            pltpu.VMEM((tok, width), bf16),
            pltpu.VMEM((n, tok, width), bf16),
            pltpu.VMEM((n, tok, part), bf16),
            pltpu.VMEM((n, tok, part), bf16),
            pltpu.VMEM((2, batch), f32),
            pltpu.VMEM((n, 2, batch), f32),
            pltpu.VMEM((n, tok, width), bf16),
            pltpu.VMEM((n, tok, width), bf16),
            pltpu.VMEM((tok, width), bf16),
            pltpu.VMEM((n, tok, width), bf16),
            pltpu.VMEM((2, rows, width), bf16),
            pltpu.SemaphoreType.DMA((slots,)),
            pltpu.SemaphoreType.DMA,
            pltpu.SemaphoreType.DMA((2,)),
            pltpu.SemaphoreType.DMA((2,)),
            pltpu.SemaphoreType.DMA((5,)),
            pltpu.SemaphoreType.DMA((5,)),
        ],
        compiler_params=pltpu.CompilerParams(
            collective_id=0, has_side_effects=True, vmem_limit_bytes=67043328
        ),
    )(features, fc_weight, centers, labels[None])
    loss = lax.dynamic_slice_in_dim(loss_row[0], lax.axis_index("cls") * tok, tok)
    grad_fc = lax.dot_general(
        columns.reshape(batch, part), all_grads.reshape(batch, width),
        (((0,), (0,)), ((), ())), preferred_element_type=f32,
    )
    return (loss, grad_centers, grad_fc)


def solution(mesh):
    placed = (P("cls", None), P(), P("cls", None), P())
    return jax.shard_map(
        on_device,
        mesh=mesh,
        in_specs=placed,
        out_specs=(P("cls"), P("cls", None), P("cls", None)),
        check_vma=False,
    )
```

time: 324 us -> 77.9 us (0.24)
  waiting for transfers between devices: 120 us -> 0 us
  blocking collectives: 118 us -> 0 us
  Pallas kernels: 0 us -> 70 us
  matrix products: 22.8 us -> 2.64 us
  other arithmetic: 19.4 us -> 0 us
  local copies, waits for them, and re-layouts: 21.7 us -> 3.28 us
  between operations: 14.2 us -> 0.65 us
  starting transfers between devices: 7.37 us -> 0 us
    reduce_scatter x1 -> x0, waiting for transfers between devices: 120 us -> none  [on_device(): lax.psum_scatter(jnp.dot(grad_cos, center_low, preferred_element_type=jnp...]
    all_gather x2 -> x0, blocking collectives: 80.9 us -> none  [the longest x1 43.2 us: on_device(): gathered = lax.all_gather(embedded, 'cls', axis=0, tiled=True)]
    pallas_call x0 -> x1, Pallas kernels: none -> 70 us  [on_device(): pl.pallas_call(functools.partial(kernel, n, rows, slots), out_shape=(jax....]
    psum x1 -> x0, blocking collectives: 37 us -> none  [on_device(): lax.psum((jnp.sum(jnp.exp(logits - logit_scale), axis=1), target_logit),...]
    dot_general x5 -> x1, matrix products: 22.8 us -> 2.64 us  [on_device(): lax.dot_general(columns.reshape(batch, part), all_grads.reshape(batch, wi...]
    unnamed x12 -> x3, local copies, waits for them, and re-layouts: 17.9 us -> 2.02 us
    convert_element_type x3 -> x0, other arithmetic: 11.1 us -> none  [the longest x1 6.77 us: on_device(): grad_cos = (logit_scale * (probs - is_target.astype(jnp.float32)) * jnp.w...]
    reduce_sum x4 -> x0, other arithmetic: 8.23 us -> none  [the longest x1 4.05 us: on_device(): jnp.sum(jnp.exp(logits - logit_scale), axis=1)]
  transfers between devices with their start and end apart: 2 -> 0, of which waited for: 1 -> 0; matrix products, arithmetic and copies ran while one was open for 17% -> 0% of each run, Pallas kernels for 0% -> 0%
where the time goes in v2:
time: 77.9 us; the launch traced here: 76.6 us
  Pallas kernels  70 us (90%)
  local copies, waits for them, and re-layouts  3.28 us (4%)
  matrix products  2.64 us (3%)
    pallas_call x1, Pallas kernels, on_device(): pl.pallas_call(functools.partial(kernel, n, rows, slots), out_shape=(jax....  70 us
    dot_general x1, matrix products, on_device(): lax.dot_general(columns.reshape(batch, part), all_grads.reshape(batch, wi...  2.64 us
    unnamed x3, local copies, waits for them, and re-layouts  2.02 us

profile of v2, /device:TPU:0, one launch (start us, length us, event | category | flops | bytes accessed | tf_op | source)
XLA Modules:
  0.0 76.6 jit_solution(7355686761736822804)
XLA Ops:
  0.6 70.0 %shard_map.67 = (f32[1,512]{1,0:T(1,128)}, bf16[4096,512]{1,0:T(8,128)(2,1)}, bf16[32,16,392]{2,1,0:T(8,128)(2,1)}, bf16[32,16,512]{2,1,0:T(8,128)(2,1)}) custom-call(bf16[16,12544]{1,0:T(8,128)(2,1)} %feat.1, bf16[12544,512]{1,0:T(8,128)(2,1)} %weight.1, bf16[4096,512]{1,0:T(8,128)(2,1)} %centers_hbm.1, s32[1,512]{1,0:T(1,128)} %bitcast.7), custom_call_target="tpu_custom_call" | custom-call | tf_op jit(solution)/shard_map/pallas_call | solution.py:231
  70.7 1.3 %dynamic-slice_bitcast_fusion = f32[16]{0:T(128)} fusion(f32[1,512]{1,0:T(1,128)} %get-tuple-element.7, s32[]{:T(128)S(6)} %select_n.3), kind=kLoop, calls=%fused_computation.1 | loop fusion | bytes 132 | tf_op jit(solution)/shard_map/dynamic_slice | solution.py:270
  72.0 0.0 copy-start
  72.0 2.6 %convolution_bitcast_fusion = f32[392,512]{1,0:T(8,128)} fusion(bf16[32,16,392]{2,1,0:T(8,128)(2,1)} %get-tuple-element.9, bf16[32,16,512]{2,1,0:T(8,128)(2,1)} %get-tuple-element.10), kind=kOutput, calls=%fused_computation | convolution fusion | flops 205520896 | bytes 1728512 | tf_op jit(solution)/shard_map/dot_general | solution.py:271
  74.6 0.0 copy-done
  74.6 2.0 %copy.12 = bf16[4096,512]{1,0:T(8,128)(2,1)} copy(bf16[4096,512]{1,0:T(8,128)(2,1)S(1)} %copy-done) | data formatting | bytes 8388608
Async XLA Ops:
  72.0 2.6 %copy-start = (bf16[4096,512]{1,0:T(8,128)(2,1)S(1)}, bf16[4096,512]{1,0:T(8,128)(2,1)}, u32[]{:S(2)}) copy-start(bf16[4096,512]{1,0:T(8,128)(2,1)} %get-tuple-element.15) | copy-start | bytes 12582916

commit v3 on v2

--- a/solution.py
+++ b/solution.py
@@ -26,10 +26,10 @@
 
 def kernel(
     n, rows, slots, feat, weight, centers_hbm, labels,
-    loss_out, gc_out, cols_out, grads_out,
+    loss_out, gc_out, fc_out,
     wbuf, cbuf, clow, inv_c, cosines, acc, esend, emb, fsend, frecv,
-    ssend, srecv, psend, precv, gsend, grecv, stage,
-    wsem, csem, osem, ksem, ssems, rsems,
+    ssend, srecv, psend, pair, precv, gsend, grecv, stage,
+    wsem, csem, osem, ssems, rsems,
 ):
     me = lax.axis_index("cls")
     tok, feats = feat.shape
@@ -40,6 +40,9 @@
     blocks = classes // rows
     part = feats // n
     half = n // 2
+    core = lax.rem(me, 2)
+    chip = me // 2
+    partner = me + 1 - 2 * core
 
     def weight_copy(c):
         return pltpu.make_async_copy(
@@ -86,11 +89,34 @@
 
         lax.fori_loop(first, last, step, 0)
 
-    def wait_all(sems, phase, target):
-        whole = target.at[pl.ds(0, n - 1)]
+    def wait_all(sems, phase, target, count):
+        whole = target.at[pl.ds(0, count)]
         pltpu.make_async_copy(whole, whole, sems.at[phase]).wait()
 
-    send_to(0, lambda dst: esend, emb, 1, n)
+    def send_chips(phase, source, target, slot):
+        def step(i, carry):
+            to = lax.rem(chip + i, half)
+            pltpu.make_async_remote_copy(
+                src_ref=source(to), dst_ref=target.at[slot],
+                send_sem=ssems.at[phase], recv_sem=rsems.at[phase],
+                device_id=(2 * to + core,), device_id_type=MESH,
+            ).start()
+            return carry
+
+        lax.fori_loop(1, half, step, 0)
+
+    def send_partner(phase, source, target):
+        def step(j, carry):
+            pltpu.make_async_remote_copy(
+                src_ref=source(j), dst_ref=target(j),
+                send_sem=ssems.at[phase], recv_sem=rsems.at[phase],
+                device_id=(partner,), device_id_type=MESH,
+            ).start()
+            return carry
+
+        lax.fori_loop(0, half, step, 0)
+
+    send_chips(0, lambda to: esend, emb, me)
 
     centers_copy.wait()
 
@@ -104,9 +130,12 @@
 
     lax.fori_loop(0, blocks, normalise, 0)
 
-    wait_all(rsems, 0, emb)
+    wait_all(rsems, 0, emb, half - 1)
+    send_partner(5, lambda j: emb.at[2 * j + core], lambda j: emb.at[2 * j + core])
     send_to(1, lambda dst: fsend.at[dst], frecv, 1, half)
     frecv[me] = fsend[me]
+    wait_all(rsems, 5, emb, half)
+    wait_all(ssems, 5, emb, half)
 
     all_emb = emb[...].reshape(batch, width).astype(f32)
     emb_low = (all_emb * inverse_norm(all_emb)).astype(bf16)
@@ -140,7 +169,7 @@
     ssend[1:2] = jnp.where(mine, tlogit, 0.0)
     srecv[me] = ssend[...]
     send_to(2, lambda dst: ssend, srecv, 1, n)
-    wait_all(rsems, 2, srecv)
+    wait_all(rsems, 2, srecv, n - 1)
     send_to(1, lambda dst: fsend.at[dst], frecv, half, n)
     stats = jnp.sum(srecv[...], axis=0)
     log_total = logit_scale + jnp.log(stats[0:1])
@@ -164,8 +193,7 @@
 
     lax.fori_loop(0, blocks, embed_grads, 0)
     psend[...] = acc[...].astype(bf16).reshape(n, tok, width)
-    precv[me] = psend[me]
-    send_to(3, lambda dst: psend.at[dst], precv, 1, n)
+    send_partner(6, lambda j: psend.at[2 * j + 1 - core], lambda j: pair.at[j])
 
     def out_copy(k, slot):
         at = pl.ds(pl.multiple_of(k * rows, rows), rows)
@@ -189,9 +217,20 @@
         out_copy(k, slot).start()
         return carry
 
-    lax.fori_loop(0, blocks, center_grads, 0)
-
-    wait_all(rsems, 3, precv)
+    lax.fori_loop(0, 1, center_grads, 0)
+    wait_all(rsems, 6, pair, half)
+
+    def add_pair(j, carry):
+        at = pl.ds(pl.multiple_of((2 * j + core) * tok, tok), tok)
+        psend[2 * j + core] = (acc[at] + pair[j].astype(f32)).astype(bf16)
+        return carry
+
+    lax.fori_loop(0, half, add_pair, 0)
+    precv[chip] = psend[me]
+    send_chips(3, lambda to: psend.at[2 * to + core], precv, chip)
+    lax.fori_loop(1, blocks, center_grads, 0)
+
+    wait_all(rsems, 3, precv, half - 1)
     grad_dir = jnp.sum(precv[...].astype(f32), axis=0)
     own = esend[...].astype(f32)
     inv_emb = inverse_norm(own)
@@ -200,20 +239,25 @@
     grad_emb = ((grad_dir - emb_dir * along) * inv_emb).astype(bf16)
     gsend[...] = grad_emb
     grecv[me] = grad_emb
-    send_to(4, lambda dst: gsend, grecv, 1, n)
-
-    wait_all(rsems, 1, frecv)
-    cols_copy = pltpu.make_async_copy(frecv, cols_out, ksem.at[0])
-    cols_copy.start()
+    send_chips(4, lambda to: gsend, grecv, me)
+
+    wait_all(rsems, 1, frecv, n - 1)
     for k in range(max(blocks - 2, 0), blocks):
         out_copy(k, k % 2).wait()
-    wait_all(rsems, 4, grecv)
-    grads_copy = pltpu.make_async_copy(grecv, grads_out, ksem.at[1])
-    grads_copy.start()
-    for phase, target in ((0, emb), (1, frecv), (2, srecv), (3, precv), (4, grecv)):
-        wait_all(ssems, phase, target)
-    cols_copy.wait()
-    grads_copy.wait()
+    wait_all(rsems, 4, grecv, half - 1)
+    send_partner(7, lambda j: grecv.at[2 * j + core], lambda j: grecv.at[2 * j + core])
+    wait_all(rsems, 7, grecv, half)
+    fc_out[...] = lax.dot_general(
+        frecv[...].reshape(batch, part), grecv[...].reshape(batch, width),
+        (((0,), (0,)), ((), ())), preferred_element_type=f32,
+    )
+    wait_all(ssems, 0, emb, half - 1)
+    wait_all(ssems, 1, frecv, n - 1)
+    wait_all(ssems, 2, srecv, n - 1)
+    wait_all(ssems, 3, precv, half - 1)
+    wait_all(ssems, 4, grecv, half - 1)
+    wait_all(ssems, 6, pair, half)
+    wait_all(ssems, 7, grecv, half)
 
 
 def on_device(features, fc_weight, centers, labels):
@@ -223,21 +267,19 @@
     batch = labels.shape[0]
     rows = min(512, 262144 // batch)
     slots = 4 if batch <= 1024 else 2
-    chunk = feats // 128 // 7 * 128
     chunk = 128 * largest_divisor(feats // 128, 14)
     part = feats // n
     vmem = pl.BlockSpec(memory_space=pltpu.VMEM)
     hbm = pl.BlockSpec(memory_space=pl.ANY)
-    loss_row, grad_centers, columns, all_grads = pl.pallas_call(
+    loss_row, grad_centers, grad_fc = pl.pallas_call(
         functools.partial(kernel, n, rows, slots),
         out_shape=(
             jax.ShapeDtypeStruct((1, batch), f32),
             jax.ShapeDtypeStruct((classes, width), bf16),
-            jax.ShapeDtypeStruct((n, tok, part), bf16),
-            jax.ShapeDtypeStruct((n, tok, width), bf16),
+            jax.ShapeDtypeStruct((part, width), f32),
         ),
         in_specs=[vmem, hbm, hbm, vmem],
-        out_specs=(vmem, hbm, hbm, hbm),
+        out_specs=(vmem, hbm, vmem),
         scratch_shapes=[
             pltpu.VMEM((slots, chunk, width), bf16),
             pltpu.VMEM((classes, width), bf16),
@@ -252,26 +294,22 @@
             pltpu.VMEM((2, batch), f32),
             pltpu.VMEM((n, 2, batch), f32),
             pltpu.VMEM((n, tok, width), bf16),
-            pltpu.VMEM((n, tok, width), bf16),
+            pltpu.VMEM((n // 2, tok, width), bf16),
+            pltpu.VMEM((n // 2, tok, width), bf16),
             pltpu.VMEM((tok, width), bf16),
             pltpu.VMEM((n, tok, width), bf16),
             pltpu.VMEM((2, rows, width), bf16),
             pltpu.SemaphoreType.DMA((slots,)),
             pltpu.SemaphoreType.DMA,
             pltpu.SemaphoreType.DMA((2,)),
-            pltpu.SemaphoreType.DMA((2,)),
-            pltpu.SemaphoreType.DMA((5,)),
-            pltpu.SemaphoreType.DMA((5,)),
+            pltpu.SemaphoreType.DMA((8,)),
+            pltpu.SemaphoreType.DMA((8,)),
         ],
         compiler_params=pltpu.CompilerParams(
             collective_id=0, has_side_effects=True, vmem_limit_bytes=67043328
         ),
     )(features, fc_weight, centers, labels[None])
     loss = lax.dynamic_slice_in_dim(loss_row[0], lax.axis_index("cls") * tok, tok)
-    grad_fc = lax.dot_general(
-        columns.reshape(batch, part), all_grads.reshape(batch, width),
-        (((0,), (0,)), ((), ())), preferred_element_type=f32,
-    )
     return (loss, grad_centers, grad_fc)
 
 

time: 77.9 us -> 63.7 us (0.82); the launches traced: 76.6 us -> 63.2 us
  Pallas kernels: 70 us -> 56 us
  local copies, waits for them, and re-layouts: 3.28 us -> 6.61 us
  matrix products: 2.64 us -> 0 us
    pallas_call x1, Pallas kernels: 70 us -> 56 us  [on_device(): pl.pallas_call(functools.partial(kernel, n, rows, slots), out_shape=(jax....]
    unnamed x3 -> x4, local copies, waits for them, and re-layouts: 2.02 us -> 5.43 us
    dot_general x1 -> x0, matrix products: 2.64 us -> none  [on_device(): lax.dot_general(columns.reshape(batch, part), all_grads.reshape(batch, wi...]
where the time goes in v3:
time: 63.7 us; the launch traced here: 63.2 us
  Pallas kernels  56 us (88%)
  local copies, waits for them, and re-layouts  6.61 us (10%)
  between operations  0.65 us (1%)
    pallas_call x1, Pallas kernels, on_device(): pl.pallas_call(functools.partial(kernel, n, rows, slots), out_shape=(jax....  56 us
    unnamed x4, local copies, waits for them, and re-layouts  5.43 us

profile of v3, /device:TPU:0, one launch (start us, length us, event | category | flops | bytes accessed | tf_op | source)
XLA Modules:
  0.0 63.2 jit_solution(2974656370171542139)
XLA Ops:
  0.6 56.0 %shard_map.67 = (f32[1,512]{1,0:T(1,128)}, bf16[4096,512]{1,0:T(8,128)(2,1)}, f32[392,512]{1,0:T(8,128)}) custom-call(bf16[16,12544]{1,0:T(8,128)(2,1)} %feat.1, bf16[12544,512]{1,0:T(8,128)(2,1)} %weight.1, bf16[4096,512]{1,0:T(8,128)(2,1)} %centers_hbm.1, s32[1,512]{1,0:T(1,128)} %bitcast.3), custom_call_target="tpu_custom_call" | custom-call | tf_op jit(solution)/shard_map/pallas_call | solution.py:274
  56.6 1.2 %dynamic-slice_bitcast_fusion = f32[16]{0:T(128)} fusion(f32[1,512]{1,0:T(1,128)} %get-tuple-element.6, s32[]{:T(128)S(6)} %select_n.3), kind=kLoop, calls=%fused_computation | loop fusion | bytes 132 | tf_op jit(solution)/shard_map/dynamic_slice | solution.py:312
  57.8 0.0 copy-start
  57.8 4.5 %copy.9 = bf16[4096,512]{1,0:T(8,128)(2,1)} copy(bf16[4096,512]{1,0:T(8,128)(2,1)} %get-tuple-element.13) | data formatting | bytes 8388608
  62.3 0.0 copy-done
  62.3 0.9 %copy.10 = f32[392,512]{1,0:T(8,128)} copy(f32[392,512]{1,0:T(8,128)S(1)} %copy-done) | data formatting | bytes 1605632
Async XLA Ops:
  57.8 4.5 %copy-start = (f32[392,512]{1,0:T(8,128)S(1)}, f32[392,512]{1,0:T(8,128)}, u32[]{:S(2)}) copy-start(f32[392,512]{1,0:T(8,128)} %get-tuple-element.14) | copy-start | bytes 2408452
